TPU v7x, 512 devices: a whole 4x8x8 slice. The times are simulated.
512 devices in a mesh: ep: 32 (over z, x), fsdp: 16 (over y, core).
Axes of the slice: x: 4, y: 8, z: 8, core: 2. Of those that a mesh axis runs over, the one named last changes fastest.
Arguments:
- train_down: float32 [64, 1408, 2048], P('ep', None, 'fsdp'), may hold values from -0.21875 to 0.21875
- other_down: float32 [64, 1408, 2048], P('ep', None, 'fsdp'), may hold values from -0.15625 to 0.15625
- router_weight: float32 [2048, 64], P('fsdp', 'ep'), may hold values from -0.125 to 0.125
- router_gain: float32 [2048], P('fsdp'), may hold values from 0.25 to 1.75
Outputs:
- ready_down: bfloat16 [64, 1408, 2048], P('ep')
- scale_down: float32 [64, 1408], P('ep')
- serve_router: bfloat16 [2048, 64], replicated
- latest_down: float32 [64, 1408, 2048], P('ep', None, 'fsdp')
All inputs are finite; a program needn't handle non-finite values.
Results may differ from a plain program's by a relative error of at most 0.001.
Values may be sent and summed in bfloat16 or wider, within the bound.
A program may use at most 128 MiB of HBM per device.

v0:
```python
import jax
import jax.numpy as jnp
from jax import lax
from jax.sharding import PartitionSpec as P


def from_everyone(x, axis):
    copies = jnp.broadcast_to(x, (lax.axis_size(axis), *x.shape))
    return lax.all_to_all(copies, axis, split_axis=0, concat_axis=0, tiled=True)


def taken_together(x, axis):
    return from_everyone(x, axis).sum(axis=0)


def laid_out(tiles, dim):
    shape = list(tiles.shape[1:])
    shape[dim] *= tiles.shape[0]
    return jnp.moveaxis(tiles, 0, dim).reshape(shape)


def gathered_copies(x, axis, dim):
    tiles = from_everyone(x, axis)
    return laid_out(tiles, dim)


def on_device(train_down, other_down, router_weight, router_gain):
    latest_down = 0.5 * other_down + 0.5 * train_down
    total_down = taken_together(jnp.sum(latest_down * latest_down, axis=2), "fsdp")
    scale_down = jnp.sqrt(total_down)
    narrow_down = (latest_down / jnp.expand_dims(scale_down, 2)).astype(jnp.bfloat16)
    ready_down = lax.all_gather(narrow_down, "fsdp", axis=2, tiled=True)
    part_router = (router_weight * router_gain[:, None]).astype(jnp.bfloat16)
    row_router = lax.all_gather(part_router, "fsdp", axis=0, tiled=True)
    serve_router = gathered_copies(row_router, "ep", 1)
    return (ready_down, scale_down, serve_router, latest_down)


def solution(mesh):
    placed = (P("ep", None, "fsdp"), P("ep", None, "fsdp"), P("fsdp", "ep"), P("fsdp"))
    return jax.shard_map(
        on_device,
        mesh=mesh,
        in_specs=placed,
        out_specs=(P("ep", None, None), P("ep", None), P(), P("ep", None, "fsdp")),
        check_vma=False,
    )
```

profile of v0, /device:TPU:1, one launch (start us, length us, event | category | flops | bytes accessed | tf_op | source)
XLA Modules:
  0.0 125.7 jit_solution(18168759618692292197)
XLA Ops:
  7.2 0.0 all-gather.2.cloned.1.call-start
  7.2 2.3 %multiply_reduce_fusion = (f32[2,1408]{1,0:T(2,128)S(1)}, f32[2,1408,128]{2,1,0:T(8,128)S(1)}) fusion(f32[2,1408,128]{2,1,0:T(8,128)} %param.5, f32[2,1408,128]{2,1,0:T(8,128)} %param.4), kind=kLoop, calls=%fused_computation.1 | loop fusion | flops 1438976 | bytes 4336640 | tf_op jit(solution)/shard_map/reduce_sum | solution.py:29
  9.5 0.0 copy-start
  9.5 19.2 %all_to_all.10 = f32[16,2,1408]{2,1,0:T(2,128)S(1)} all-to-all(f32[16,2,1408]{2,1,0:T(2,128)S(1)} %broadcast_in_dim.8), channel_id=1, replica_groups=mesh['ep'=32,'fsdp'=16] {'fsdp'}, dimensions={0} | all-to-all | bytes 360448 | tf_op jit(solution)/shard_map/all_to_all | solution.py:9
  28.7 0.1 reduce_sum.19
  28.8 0.0 copy-start.1
  28.8 0.0 copy-start.2
  28.8 0.0 copy-start.3
  28.8 1.3 %divide_convert_fusion = bf16[2,1408,128]{2,1,0:T(8,128)(2,1)} fusion(f32[2,1408,128]{2,1,0:T(8,128)S(1)} %get-tuple-element.13, f32[2,1408]{1,0:T(2,128)S(1)} %sqrt.7), kind=kLoop, calls=%fused_computation | loop fusion | flops 720896 | bytes 2173952 | tf_op jit(solution)/shard_map/convert_element_type | solution.py:31
  30.1 0.0 copy-done
  30.1 0.0 all-gather.2.cloned.1.call-update
  30.2 0.0 copy-done.1
  30.2 0.0 copy-done.2
  30.2 0.0 copy-done.3
  30.2 14.5 %all_gather.7 = bf16[2048,2]{0,1:T(2,128)(2,1)S(1)} all-gather(bf16[128,2]{0,1:T(2,128)(2,1)S(1)} %multiply_convert_fusion), channel_id=1, replica_groups=mesh['ep'=32,'fsdp'=16] {'fsdp'}, dimensions={0}, use_global_device_ids=true | all-gather | bytes 8704 | tf_op jit(solution)/shard_map/all_gather | solution.py:34
  44.7 0.1 broadcast_in_dim.9
  44.8 23.3 %all_to_all.11 = bf16[32,2048,2]{1,2,0:T(2,128)(2,1)S(1)} all-to-all(bf16[32,2048,2]{1,2,0:T(2,128)(2,1)S(1)} %broadcast_in_dim.9), channel_id=1, replica_groups=mesh['ep'=32,'fsdp'=16] {'ep'}, dimensions={0} | all-to-all | bytes 524288 | tf_op jit(solution)/shard_map/all_to_all | solution.py:9
  68.1 0.8 reshape.15
  68.9 39.8 %all-gather.2.cloned.1.call-done = bf16[2,1408,2048]{2,1,0:T(8,128)(2,1)} async-done(((bf16[2,1408,128]{2,1,0:T(8,128)(2,1)}), bf16[2,1408,2048]{2,1,0:T(8,128)(2,1)}) %all-gather.2.cloned.1.call-update) | async-done | bytes 11534352 | tf_op jit(solution)/shard_map/all_gather | solution.py:32
  108.7 10.1 %copy.11 = bf16[2,1408,2048]{2,1,0:T(8,128)(2,1)} copy(bf16[2,1408,2048]{2,1,0:T(8,128)(2,1)} %all-gather.2.cloned.1.call-done) | data formatting | bytes 23068672
  (3 shorter events, 0.1 us)
Async XLA Ops:
  7.2 101.6 %all-gather.2.cloned.1.call-start = ((), (), s32[]{:S(2)}) async-start(), calls=%async_computation.2 | async-start | bytes 12255232 | tf_op jit(solution)/shard_map/all_gather | solution.py:32
  9.5 20.7 %copy-start = (f32[2,1408,128]{2,1,0:T(8,128)}, f32[2,1408,128]{2,1,0:T(8,128)S(1)}, u32[]{:S(2)}) copy-start(f32[2,1408,128]{2,1,0:T(8,128)S(1)} %get-tuple-element.13) | copy-start | bytes 4325380
  28.8 1.4 %copy-start.1 = (f32[2,1408]{1,0:T(2,128)}, f32[2,1408]{1,0:T(2,128)S(1)}, u32[]{:S(2)}) copy-start(f32[2,1408]{1,0:T(2,128)S(1)} %sqrt.7) | copy-start | bytes 33796
  28.8 1.4 %copy-start.2 = (f32[128,2]{0,1:T(2,128)S(1)}, f32[128,2]{0,1:T(2,128)}, u32[]{:S(2)}) copy-start(f32[128,2]{0,1:T(2,128)} %param.6) | copy-start | bytes 3076
  28.8 1.4 %copy-start.3 = (f32[128]{0:T(128)S(1)}, f32[128]{0:T(128)}, u32[]{:S(2)}) copy-start(f32[128]{0:T(128)} %param.7) | copy-start | bytes 1540
Sparse Core Ops, SparseCore 0:
  30.3 78.3 all-gather.1
where the time goes:
time: 126 us
  blocking collectives  57 us (45%)
  waiting for transfers between devices  39.8 us (32%)
  between operations  14.1 us (11%)
  local copies, waits for them, and re-layouts  11.1 us (9%)
  other arithmetic  3.63 us (3%)
    all_to_all x2, blocking collectives, from_everyone(): return lax.all_to_all(copies, axis, split_axis=0, concat_axis=0, tiled=True)  42.5 us
    all_gather x1, waiting for transfers between devices, on_device(): ready_down = lax.all_gather(narrow_down, 'fsdp', axis=2, tiled=True)  39.8 us
    all_gather x1, blocking collectives, on_device(): row_router = lax.all_gather(part_router, 'fsdp', axis=0, tiled=True)  14.5 us
    unnamed x9, local copies, waits for them, and re-layouts  10.1 us
  transfers between devices with their start and end apart: 1, of which 1 were waited for; matrix products, arithmetic and copies ran while one was open for 1% of the time, Pallas kernels for 0%

commit v1 on v0

--- a/solution.py
+++ b/solution.py
@@ -31,7 +31,9 @@
     narrow_down = (latest_down / jnp.expand_dims(scale_down, 2)).astype(jnp.bfloat16)
     ready_down = lax.all_gather(narrow_down, "fsdp", axis=2, tiled=True)
     part_router = (router_weight * router_gain[:, None]).astype(jnp.bfloat16)
-    row_router = lax.all_gather(part_router, "fsdp", axis=0, tiled=True)
+    row_router = jnp.concatenate(
+        lax.all_to_all(jnp.stack([part_router] * lax.axis_size("fsdp")), "fsdp", 0, 0), axis=0
+    )
     serve_router = gathered_copies(row_router, "ep", 1)
     return (ready_down, scale_down, serve_router, latest_down)
 

time: 126 us -> 126 us (level)
  blocking collectives: 57 us -> 52 us
  waiting for transfers between devices: 39.8 us -> 44.7 us
    all_gather x1 -> x0, blocking collectives: 14.5 us -> none  [on_device(): row_router = lax.all_gather(part_router, 'fsdp', axis=0, tiled=True)]
    all_to_all x0 -> x1, blocking collectives: none -> 9.77 us  [on_device(): lax.all_to_all(jnp.stack([part_router] * lax.axis_size('fsdp')), 'fsdp',...]
    all_gather x1, waiting for transfers between devices: 39.8 us -> 44.7 us  [on_device(): ready_down = lax.all_gather(narrow_down, 'fsdp', axis=2, tiled=True)]
where the time goes in v1:
time: 126 us
  blocking collectives  52 us (41%)
  waiting for transfers between devices  44.7 us (35%)
  between operations  14.1 us (11%)
  local copies, waits for them, and re-layouts  11.1 us (9%)
  other arithmetic  3.63 us (3%)
    all_gather x1, waiting for transfers between devices, on_device(): ready_down = lax.all_gather(narrow_down, 'fsdp', axis=2, tiled=True)  44.7 us
    all_to_all x2, blocking collectives, from_everyone(): return lax.all_to_all(copies, axis, split_axis=0, concat_axis=0, tiled=True)  42.3 us
    unnamed x9, local copies, waits for them, and re-layouts  10.1 us
    all_to_all x1, blocking collectives, on_device(): lax.all_to_all(jnp.stack([part_router] * lax.axis_size('fsdp')), 'fsdp',...  9.77 us
  transfers between devices with their start and end apart: 1, of which 1 were waited for; matrix products, arithmetic and copies ran while one was open for 1% of the time, Pallas kernels for 0%

profile of v1, /device:TPU:1, one launch (start us, length us, event | category | flops | bytes accessed | tf_op | source)
XLA Modules:
  0.0 125.7 jit_solution(15134980987610731615)
XLA Ops:
  7.2 0.0 all-gather.2.cloned.1.call-start
  7.2 2.3 %multiply_reduce_fusion = (f32[2,1408]{1,0:T(2,128)S(1)}, f32[2,1408,128]{2,1,0:T(8,128)S(1)}) fusion(f32[2,1408,128]{2,1,0:T(8,128)} %param.5, f32[2,1408,128]{2,1,0:T(8,128)} %param.4), kind=kLoop, calls=%fused_computation.1 | loop fusion | flops 1438976 | bytes 4336640 | tf_op jit(solution)/shard_map/reduce_sum | solution.py:29
  9.5 0.0 copy-start
  9.5 19.2 %all_to_all.15 = f32[16,2,1408]{2,1,0:T(2,128)S(1)} all-to-all(f32[16,2,1408]{2,1,0:T(2,128)S(1)} %broadcast_in_dim.8), channel_id=1, replica_groups=mesh['ep'=32,'fsdp'=16] {'fsdp'}, dimensions={0} | all-to-all | bytes 360448 | tf_op jit(solution)/shard_map/all_to_all | solution.py:9
  28.7 0.1 reduce_sum.19
  28.8 0.0 copy-start.1
  28.8 0.0 copy-start.2
  28.8 0.0 copy-start.3
  28.8 1.3 %divide_convert_fusion = bf16[2,1408,128]{2,1,0:T(8,128)(2,1)} fusion(f32[2,1408,128]{2,1,0:T(8,128)S(1)} %get-tuple-element.13, f32[2,1408]{1,0:T(2,128)S(1)} %sqrt.7), kind=kLoop, calls=%fused_computation | loop fusion | flops 720896 | bytes 2173952 | tf_op jit(solution)/shard_map/convert_element_type | solution.py:31
  30.1 0.0 copy-done
  30.1 0.0 all-gather.2.cloned.1.call-update
  30.2 0.0 copy-done.1
  30.2 0.0 copy-done.2
  30.2 0.0 copy-done.3
  30.2 9.8 %all_to_all.16 = bf16[16,128,2]{1,2,0:T(2,128)(2,1)S(1)} all-to-all(bf16[16,128,2]{1,2,0:T(2,128)(2,1)S(1)} %stack.2), channel_id=1, replica_groups=mesh['ep'=32,'fsdp'=16] {'fsdp'}, dimensions={0} | all-to-all | bytes 16384 | tf_op jit(solution)/shard_map/all_to_all | solution.py:35
  40.0 0.1 broadcast_in_dim.9
  40.1 23.1 %all_to_all.17 = bf16[32,2048,2]{1,2,0:T(2,128)(2,1)S(1)} all-to-all(bf16[32,2048,2]{1,2,0:T(2,128)(2,1)S(1)} %broadcast_in_dim.9), channel_id=1, replica_groups=mesh['ep'=32,'fsdp'=16] {'ep'}, dimensions={0} | all-to-all | bytes 524288 | tf_op jit(solution)/shard_map/all_to_all | solution.py:9
  63.2 0.8 reshape.21
  64.0 44.7 %all-gather.2.cloned.1.call-done = bf16[2,1408,2048]{2,1,0:T(8,128)(2,1)} async-done(((bf16[2,1408,128]{2,1,0:T(8,128)(2,1)}), bf16[2,1408,2048]{2,1,0:T(8,128)(2,1)}) %all-gather.2.cloned.1.call-update) | async-done | bytes 11534352 | tf_op jit(solution)/shard_map/all_gather | solution.py:32
  108.7 10.1 %copy.11 = bf16[2,1408,2048]{2,1,0:T(8,128)(2,1)} copy(bf16[2,1408,2048]{2,1,0:T(8,128)(2,1)} %all-gather.2.cloned.1.call-done) | data formatting | bytes 23068672
  (4 shorter events, 0.1 us)
Async XLA Ops:
  7.2 101.6 %all-gather.2.cloned.1.call-start = ((), (), s32[]{:S(2)}) async-start(), calls=%async_computation.3 | async-start | bytes 12255232 | tf_op jit(solution)/shard_map/all_gather | solution.py:32
  9.5 20.7 %copy-start = (f32[2,1408,128]{2,1,0:T(8,128)}, f32[2,1408,128]{2,1,0:T(8,128)S(1)}, u32[]{:S(2)}) copy-start(f32[2,1408,128]{2,1,0:T(8,128)S(1)} %get-tuple-element.13) | copy-start | bytes 4325380
  28.8 1.4 %copy-start.1 = (f32[2,1408]{1,0:T(2,128)}, f32[2,1408]{1,0:T(2,128)S(1)}, u32[]{:S(2)}) copy-start(f32[2,1408]{1,0:T(2,128)S(1)} %sqrt.7) | copy-start | bytes 33796
  28.8 1.4 %copy-start.2 = (f32[128,2]{0,1:T(2,128)S(1)}, f32[128,2]{0,1:T(2,128)}, u32[]{:S(2)}) copy-start(f32[128,2]{0,1:T(2,128)} %param.6) | copy-start | bytes 3076
  28.8 1.4 %copy-start.3 = (f32[128]{0:T(128)S(1)}, f32[128]{0:T(128)}, u32[]{:S(2)}) copy-start(f32[128]{0:T(128)} %param.7) | copy-start | bytes 1540
Sparse Core Ops, SparseCore 0:
  30.3 78.3 all-gather.1
